TPU v7x, 32 devices: a whole 2x2x4 slice. The times are simulated.
32 devices in a mesh: grp: 4 (over y, x), dev: 8 (over z, core).
Axes of the slice: x: 2, y: 2, z: 4, core: 2. Of those that a mesh axis runs over, the one named last changes fastest.
Arguments:
- table: bfloat16 [8, 32768, 256], P('grp', 'dev'), may hold values from -0.75 to 0.75
- token_ids: int32 [8192], P(('grp', 'dev')), may hold values from 0 to 32767, as said below
- hidden: bfloat16 [8192, 2560], P(('grp', 'dev')), may hold values from -6 to 6
- w_proj: bfloat16 [2560, 2048], replicated, may hold values from -0.125 to 0.125
- norm_gain: float32 [256], replicated, may hold values from 0.5 to 1.5
Outputs:
- served_table: bfloat16 [8, 4, 1024, 2048], P('dev', 'grp')
- layer_inputs: bfloat16 [8192, 8, 256], P(('grp', 'dev'))
Inputs may be any that keep to these rules, and one draw needn't show every extreme that they name: `token_ids`: of the 256 tokens of one device, at most 16 have ids in any one aligned block of 1024 vocabulary rows, and exactly 16 in some block.
All inputs are finite; a program needn't handle non-finite values.
Results may differ from a plain program's by a relative error of at most 0.001.
Values may be sent and summed in bfloat16 or wider, within the bound.
A program may use at most 128 MiB of HBM per device.

v0:
```python
import functools
import math

import jax
import jax.numpy as jnp
from jax import lax
from jax.experimental import pallas as pl
from jax.experimental.pallas import tpu as pltpu
from jax.sharding import PartitionSpec as P

MESH = pl.DeviceIdType.MESH
LANES = 128
PIECES = 4


def column(row):
    return jnp.transpose(jnp.broadcast_to(row.astype(jnp.float32), (LANES, LANES)))


def exchange(n_grp, n_dev, cap,
             ids_ref, want_ref, hidden_hbm, gain_hbm, table_ref, w_ref,
             served_ref, out_ref,
             hidden_ref, gain_ref, tbl, wbuf, ids_buf, want_buf, cols, send, recv, esend, erecv, mix,
             ids_ss, ids_rs, want_ss, want_rs, tab_ss, tab_rs, z_ss, z_rs, e_ss, e_rs,
             tbl_sem, w_sem, hidden_sem, gain_sem, own_sem):
    g = lax.axis_index("grp")
    d = lax.axis_index("dev")
    layer_share, vocab_share, width = table_ref.shape
    rows = vocab_share // n_grp
    tok = hidden_ref.shape[0]
    layers = layer_share * n_grp
    wide = layer_share * width
    slots = n_grp * cap
    all_slots = n_dev * slots

    def grp_at(i):
        return lax.rem(g + i, n_grp)

    def dev_at(j):
        return lax.rem(d + j, n_dev)

    load_table = pltpu.make_async_copy(table_ref, tbl, tbl_sem)
    load_table.start()
    load_w = pltpu.make_async_copy(w_ref, wbuf, w_sem)
    load_w.start()
    load_hidden = pltpu.make_async_copy(hidden_hbm, hidden_ref, hidden_sem)
    load_hidden.start()
    load_gain = pltpu.make_async_copy(gain_hbm, gain_ref, gain_sem)
    load_gain.start()

    barrier = pltpu.get_barrier_semaphore()
    for i in range(n_grp):
        def greet(j, carry, i=i):
            pl.semaphore_signal(
                barrier, inc=1, device_id={"grp": grp_at(i), "dev": dev_at(j)}, device_id_type=MESH
            )
            return carry
        lax.fori_loop(1 if i == 0 else 0, n_dev, greet, 0)
    pl.semaphore_wait(barrier, n_grp * n_dev - 1)

    def ids_copy(i, j):
        return pltpu.make_async_remote_copy(
            src_ref=ids_ref.at[dev_at(j)], dst_ref=ids_buf.at[g, d],
            send_sem=ids_ss.at[i, j], recv_sem=ids_rs.at[i, j],
            device_id={"grp": grp_at(i), "dev": dev_at(j)}, device_id_type=MESH,
        )

    def want_copy(i):
        return pltpu.make_async_remote_copy(
            src_ref=want_ref, dst_ref=want_buf.at[g],
            send_sem=want_ss.at[i], recv_sem=want_rs.at[i],
            device_id={"grp": grp_at(i), "dev": d}, device_id_type=MESH,
        )

    order = list(range(n_grp - 1, 0, -1)) + [0]
    for i in [(n_grp - o) % n_grp for o in order]:
        def start_ids(j, carry, i=i):
            ids_copy(i, j).start()
            return carry
        lax.fori_loop(1 if i == 0 else 0, n_dev, start_ids, 0)
    for i in range(1, n_grp):
        want_copy(i).start()

    part = rows // PIECES
    pieces = [(l, p) for l in range(layer_share) for p in range(PIECES)]

    def tab_copy(i, l, p):
        gp = grp_at(i)
        return pltpu.make_async_remote_copy(
            src_ref=table_ref.at[l, pl.ds(pl.multiple_of(gp * rows + p * part, part), part), :],
            dst_ref=served_ref.at[
                pl.ds(p * part, part),
                pl.ds(pl.multiple_of((g * layer_share + l) * width, width), width),
            ],
            send_sem=tab_ss.at[i, l, p], recv_sem=tab_rs.at[i, l, p],
            device_id={"grp": gp, "dev": d}, device_id_type=MESH,
        )

    def start_pieces(first, last):
        for l, p in pieces[first:last]:
            for i in range(1, n_grp):
                tab_copy(i, l, p).start()

    ahead = len(pieces) * 7 // 8
    start_pieces(0, ahead)

    def own_copy(l):
        return pltpu.make_async_copy(
            table_ref.at[l, pl.ds(pl.multiple_of(g * rows, rows), rows), :],
            served_ref.at[:, pl.ds(pl.multiple_of((g * layer_share + l) * width, width), width)],
            own_sem.at[l],
        )

    for l in range(layer_share):
        own_copy(l).start()
    load_table.wait()

    ids_buf[g, d] = ids_ref[d]
    want_buf[g] = want_ref[...]

    def z_copy(o, j):
        dp = dev_at(j)
        gp = grp_at(o)
        return pltpu.make_async_remote_copy(
            src_ref=send.at[o, dp],
            dst_ref=recv.at[gp, pl.ds(pl.multiple_of(d * slots, slots), slots), :],
            send_sem=z_ss.at[o, j], recv_sem=z_rs.at[o, j],
            device_id={"grp": g, "dev": dp}, device_id_type=MESH,
        )

    for o in order:
        gp = grp_at(o)
        back = (n_grp - o) % n_grp

        def take_ids(j, carry, back=back):
            ids_copy(back, j).wait_recv()
            return carry
        lax.fori_loop(1 if back == 0 else 0, n_dev, take_ids, 0)

        def turn(a, carry, gp=gp):
            cols[a] = column(ids_buf[gp, a])
            return carry
        lax.fori_loop(0, n_dev, turn, 0)

        def block(b, carry, o=o):
            at = pl.multiple_of(b * cap, cap)
            wanted = cols[:, pl.ds(at, cap), :].reshape(n_dev * cap, LANES)
            lane = lax.broadcasted_iota(jnp.int32, (n_dev * cap, LANES), 1)
            lane = (lane + (d * n_grp + b) * rows).astype(jnp.float32)
            wanted = wanted - lane
            hit = jnp.concatenate(
                [(wanted == float(c * LANES)).astype(jnp.float32) for c in range(rows // LANES)], axis=1
            ).astype(jnp.bfloat16)
            for l in range(layer_share):
                found = jnp.dot(
                    hit, tbl[l, pl.ds(pl.multiple_of(b * rows, rows), rows), :],
                    preferred_element_type=jnp.float32,
                ).astype(jnp.bfloat16)
                send[o, :, pl.ds(at, cap), l * width:(l + 1) * width] = found.reshape(n_dev, cap, width)
            return carry
        lax.fori_loop(0, n_grp, block, 0)

        def start_z(j, carry, o=o):
            z_copy(o, j).start()
            return carry
        lax.fori_loop(1, n_dev, start_z, 0)
        recv[gp, pl.ds(pl.multiple_of(d * slots, slots), slots), :] = send[o, d]

    load_w.wait()
    load_hidden.wait()
    load_gain.wait()

    def project(l):
        proj = jnp.dot(hidden_ref[...], wbuf[:, l * width:(l + 1) * width], preferred_element_type=jnp.float32)
        mean_sq = jnp.mean(proj * proj, axis=-1, keepdims=True)
        return proj / jnp.sqrt(mean_sq + 1e-06) * gain_ref[...]

    for l in range(layers):
        mix[:, l, :] = project(l)

    def e_copy(o):
        return pltpu.make_async_remote_copy(
            src_ref=esend.at[o], dst_ref=erecv.at[g],
            send_sem=e_ss.at[o], recv_sem=e_rs.at[o],
            device_id={"grp": grp_at(o), "dev": d}, device_id_type=MESH,
        )

    for o in order:
        gp = grp_at(o)
        if o:
            want_copy(n_grp - o).wait_recv()

        def take_rows(j, carry, o=o):
            z_copy(o, j).wait_recv()
            return carry
        lax.fori_loop(1, n_dev, take_rows, 0)

        for t in range(tok // LANES):
            mine = column(want_buf[gp, t:t + 1, :])
            lane = lax.broadcasted_iota(jnp.int32, (LANES, LANES), 1).astype(jnp.float32)
            mine = mine - lane
            picker = jnp.concatenate(
                [(mine == float(c * LANES)).astype(jnp.float32) for c in range(all_slots // LANES)], axis=1
            ).astype(jnp.bfloat16)
            picked = jnp.dot(picker, recv[gp], preferred_element_type=jnp.float32).astype(jnp.bfloat16)
            if o:
                esend[o, t * LANES:(t + 1) * LANES, :] = picked
            else:
                erecv[g, t * LANES:(t + 1) * LANES, :] = picked
        if o:
            e_copy(o).start()
        if o == order[-2]:
            start_pieces(ahead, len(pieces))

    for o in range(1, n_grp):
        e_copy(o).wait_recv()

    for l in range(layers):
        at = (l % layer_share) * width
        emb = erecv[l // layer_share, :, at:at + width].astype(jnp.float32)
        mix[:, l, :] = (mix[:, l, :] + math.sqrt(width) * emb) / math.sqrt(2.0)
    out_ref[...] = mix[...].astype(jnp.bfloat16)

    for l in range(layer_share):
        own_copy(l).wait()
    for l, p in pieces:
        for i in range(1, n_grp):
            tab_copy(i, l, p).wait()
    for i in range(n_grp):
        def end_ids(j, carry, i=i):
            ids_copy(i, j).wait_send()
            return carry
        lax.fori_loop(1 if i == 0 else 0, n_dev, end_ids, 0)

        def end_z(j, carry, i=i):
            z_copy(i, j).wait_send()
            return carry
        lax.fori_loop(1, n_dev, end_z, 0)
        if i:
            want_copy(i).wait_send()
            e_copy(i).wait_send()


def on_device(table, token_ids, hidden, w_proj, norm_gain):
    n_grp = lax.axis_size("grp")
    n_dev = lax.axis_size("dev")
    layer_share, vocab_share, width = table.shape
    layers = layer_share * n_grp
    tok = token_ids.shape[0]
    rows = vocab_share // n_grp
    blocks = n_grp * n_dev
    cap = -(-max(2, 2 * tok // blocks) // 16) * 16
    slots = n_grp * cap
    assert slots <= LANES and tok % LANES == 0 and rows % LANES == 0
    wide = layer_share * width

    owner = token_ids // rows
    positions = jnp.arange(tok, dtype=jnp.int32)
    same = owner[:, None] == owner[None, :]
    earlier = positions[None, :] < positions[:, None]
    slot = jnp.sum((same & earlier).astype(jnp.int32), axis=1)
    wanted = owner * cap + slot
    hit = (wanted[:, None] == jnp.arange(blocks * cap, dtype=jnp.int32)[None, :]).astype(jnp.int32)
    outgoing = jnp.sum(hit * (token_ids + 1)[:, None], axis=0) - 1
    outgoing = outgoing.reshape(n_dev, 1, slots)
    outgoing = jnp.pad(outgoing, ((0, 0), (0, 0), (0, LANES - slots)), constant_values=-1)

    vmem = pl.BlockSpec(memory_space=pltpu.VMEM)
    hbm = pl.BlockSpec(memory_space=pltpu.HBM)
    dma = pltpu.SemaphoreType.DMA
    bf16 = jnp.bfloat16
    served, mixed = pl.pallas_call(
        functools.partial(exchange, n_grp, n_dev, cap),
        out_shape=(
            pltpu.VMEM((rows, layers * width), bf16),
            pltpu.VMEM((tok, layers, width), bf16),
        ),
        in_specs=[vmem, vmem, hbm, hbm, hbm, hbm],
        out_specs=(vmem, vmem),
        scratch_shapes=[
            pltpu.VMEM(hidden.shape, bf16),
            pltpu.VMEM((1, width), jnp.float32),
            pltpu.VMEM(table.shape, bf16),
            pltpu.VMEM(w_proj.shape, bf16),
            pltpu.VMEM((n_grp, n_dev, 1, LANES), jnp.int32),
            pltpu.VMEM((n_grp, tok // LANES, LANES), jnp.int32),
            pltpu.VMEM((n_dev, LANES, LANES), jnp.float32),
            pltpu.VMEM((n_grp, n_dev, slots, wide), bf16),
            pltpu.VMEM((n_grp, n_dev * slots, wide), bf16),
            pltpu.VMEM((n_grp, tok, wide), bf16),
            pltpu.VMEM((n_grp, tok, wide), bf16),
            pltpu.VMEM((tok, layers, width), jnp.float32),
            dma((n_grp, n_dev)), dma((n_grp, n_dev)),
            dma((n_grp,)), dma((n_grp,)),
            dma((n_grp, layer_share, PIECES)), dma((n_grp, layer_share, PIECES)),
            dma((n_grp, n_dev)), dma((n_grp, n_dev)),
            dma((n_grp,)), dma((n_grp,)),
            dma, dma, dma, dma, dma((layer_share,)),
        ],
        compiler_params=pltpu.CompilerParams(
            collective_id=0, has_side_effects=True, vmem_limit_bytes=44 * 2**20
        ),
        name="exchange",
    )(outgoing, wanted.reshape(tok // LANES, LANES), hidden, norm_gain.reshape(1, width), table, w_proj)
    return (served.reshape(1, 1, rows, layers * width), mixed)


def solution(mesh):
    in_specs = (P("grp", "dev", None), P(("grp", "dev")), P(("grp", "dev"), None), P(), P())
    out_specs = (P("dev", "grp", None, None), P(("grp", "dev"), None, None))
    return jax.shard_map(
        on_device, mesh=mesh, in_specs=in_specs, out_specs=out_specs, check_vma=False
    )
```

profile of v0, /device:TPU:25, one launch (start us, length us, event | category | flops | bytes accessed | tf_op | source)
XLA Modules:
  0.0 73.8 jit_solution(11268477599767418397)
XLA Ops:
  0.6 0.7 and_select_fusion
  1.3 0.2 convert_reduce_fusion
  1.5 0.2 select_reduce_fusion
  1.7 0.1 sub.14
  1.8 0.0 copy-start
  1.8 1.3 %copy-done = bf16[256,2560]{1,0:T(8,128)(2,1)S(1)} copy-done((bf16[256,2560]{1,0:T(8,128)(2,1)S(1)}, bf16[256,2560]{1,0:T(8,128)(2,1)}, u32[]{:S(2)}) %copy-start) | copy-done | bytes 1310744
  3.1 0.0 copy-start.1
  3.1 0.7 copy-done.1
  3.8 67.1 %exchange.1 = (bf16[1024,2048]{1,0:T(8,128)(2,1)S(1)}, bf16[256,8,256]{2,1,0:T(8,128)(2,1)S(1)}) custom-call(s32[8,1,128]{2,1,0:T(1,128)S(1)} %pad.4.ids_ref, s32[2,128]{1,0:T(2,128)S(1)} %bitcast.4, bf16[256,2560]{1,0:T(8,128)(2,1)S(1)} %copy-done, f32[1,256]{1,0:T(1,128)S(1)} %bitcast.5, bf16[2,4096,256]{2,1,0:T(8,128)(2,1)} %table_ref.1, ...), custom_call_target="tpu_custom_call" | custom-call | tf_op jit(solution)/shard_map/exchange/pallas_call | solution.py:272
  70.8 2.0 %copy.9 = bf16[1,1,1024,2048]{3,2,1,0:T(8,128)(2,1)} copy(bf16[1,1,1024,2048]{3,2,1,0:T(8,128)(2,1)S(1)} %bitcast.3) | data formatting | bytes 8388608
  72.9 1.0 %copy.10 = bf16[256,8,256]{2,1,0:T(8,128)(2,1)} copy(bf16[256,8,256]{2,1,0:T(8,128)(2,1)S(1)} %get-tuple-element.9) | data formatting | bytes 2097152
  (3 shorter events, 0.0 us)
Async XLA Ops:
  1.8 1.3 %copy-start = (bf16[256,2560]{1,0:T(8,128)(2,1)S(1)}, bf16[256,2560]{1,0:T(8,128)(2,1)}, u32[]{:S(2)}) copy-start(bf16[256,2560]{1,0:T(8,128)(2,1)} %hidden_hbm.1) | copy-start | bytes 3932164
  3.1 0.7 copy-start.1
where the time goes:
time: 75.2 us; the launch traced here: 73.8 us
  Pallas kernels  67.1 us (89%)
  local copies, waits for them, and re-layouts  5.07 us (7%)
  other arithmetic  1.03 us (1%)
    pallas_call x1, Pallas kernels, on_device(): pl.pallas_call(functools.partial(exchange, n_grp, n_dev, cap), out_shape=...  67.1 us
    unnamed x6, local copies, waits for them, and re-layouts  4.98 us

commit v1 on v0

v1 whole, which is shorter than its diff:
```python
import functools
import math

import jax
import jax.numpy as jnp
from jax import lax
from jax.experimental import pallas as pl
from jax.experimental.pallas import tpu as pltpu
from jax.sharding import PartitionSpec as P

MESH = pl.DeviceIdType.MESH
LANES = 128
PIECES = 8
SPLIT = (10, 12, 14)


def column(row):
    return jnp.transpose(jnp.broadcast_to(row, (LANES, LANES)))


def exchange(n_grp, n_dev, cap,
             ids_hbm, hidden_hbm, gain_hbm, table_ref, w_ref,
             served_ref, out_ref,
             ids_ref, hidden_ref, gain_ref, tbl, wbuf, want_buf, req_send, req_buf, merged,
             send, recv, esend, erecv, mix,
             want_ss, want_rs, req_ss, req_rs, mrg_ss, mrg_rs, tab_ss, tab_rs, z_ss, z_rs, e_ss, e_rs,
             ids_sem, tbl_sem, w_sem, hidden_sem, gain_sem, own_sem):
    g = lax.axis_index("grp")
    d = lax.axis_index("dev")
    layer_share, vocab_share, width = table_ref.shape
    rows = vocab_share // n_grp
    tok = hidden_ref.shape[0]
    halves = tok // LANES
    layers = layer_share * n_grp
    blocks = n_grp * n_dev
    slots = n_grp * cap
    all_slots = n_dev * slots
    groups = n_dev * cap // LANES
    half_grp = n_grp // 2
    f32 = jnp.float32
    bf16 = jnp.bfloat16

    def grp_at(i):
        return lax.rem(g // 2 + i // 2, half_grp) * 2 + lax.rem(g % 2 + i % 2, 2)

    def back(i):
        return ((half_grp - i // 2) % half_grp) * 2 + i % 2

    def dev_at(j):
        return lax.rem(d + j, n_dev)

    def to_grp(i):
        return dict(device_id={"grp": grp_at(i), "dev": d}, device_id_type=MESH)

    def to_dev(j):
        return dict(device_id={"grp": g, "dev": dev_at(j)}, device_id_type=MESH)

    order = list(range(n_grp - 1, -1, -1))

    barrier = pltpu.get_barrier_semaphore()
    for i in range(1, n_grp):
        pl.semaphore_signal(barrier, inc=1, **to_grp(i))

    def greet(j, carry):
        pl.semaphore_signal(barrier, inc=1, **to_dev(j))
        return carry
    lax.fori_loop(1, n_dev, greet, 0)

    load_ids = pltpu.make_async_copy(ids_hbm, ids_ref, ids_sem)
    load_ids.start()
    load_table = pltpu.make_async_copy(table_ref, tbl, tbl_sem)
    load_table.start()
    load_w = pltpu.make_async_copy(w_ref, wbuf, w_sem)
    load_w.start()
    load_hidden = pltpu.make_async_copy(hidden_hbm, hidden_ref, hidden_sem)
    load_hidden.start()
    load_gain = pltpu.make_async_copy(gain_hbm, gain_ref, gain_sem)
    load_gain.start()

    part = rows // PIECES
    pieces = [(l, p) for l in range(layer_share) for p in range(PIECES)]

    def tab_copy(i, l, p):
        gp = grp_at(i)
        return pltpu.make_async_remote_copy(
            src_ref=table_ref.at[l, pl.ds(pl.multiple_of(gp * rows + p * part, part), part), :],
            dst_ref=served_ref.at[
                pl.ds(p * part, part),
                pl.ds(pl.multiple_of((g * layer_share + l) * width, width), width),
            ],
            send_sem=tab_ss.at[i, l, p], recv_sem=tab_rs.at[i, l, p], **to_grp(i),
        )

    cuts = [0] + [len(pieces) * s // 16 for s in SPLIT] + [len(pieces)]

    def start_pieces(k):
        for l, p in pieces[cuts[k]:cuts[k + 1]]:
            for i in range(n_grp - 1, 0, -1):
                tab_copy(i, l, p).start()

    def own_copy(l):
        return pltpu.make_async_copy(
            table_ref.at[l, pl.ds(pl.multiple_of(g * rows, rows), rows), :],
            served_ref.at[:, pl.ds(pl.multiple_of((g * layer_share + l) * width, width), width)],
            own_sem.at[l],
        )

    pl.semaphore_wait(barrier, n_grp - 1 + n_dev - 1)
    start_pieces(0)

    load_ids.wait()
    lane = lax.broadcasted_iota(jnp.int32, (LANES, LANES), 1).astype(f32)
    sub = lax.broadcasted_iota(jnp.int32, (LANES, LANES), 0).astype(f32)
    id_row = [ids_ref[h:h + 1, :].astype(f32) for h in range(halves)]
    id_col = [column(r) for r in id_row]

    def owner_of(v):
        return jnp.floor((v + 0.5) * (1.0 / rows))

    own_row = [owner_of(r) for r in id_row]
    own_col = [owner_of(c) for c in id_col]
    slot_col = []
    for h in range(halves):
        by_lane = jnp.zeros((LANES, LANES), f32)
        by_sub = jnp.zeros((LANES, LANES), f32)
        for k in range(h + 1):
            same = own_col[h] == own_row[k]
            also = own_col[k] == own_row[h]
            if k == h:
                same = same & (lane < sub)
                also = also & (sub < lane)
            by_lane = by_lane + jnp.where(same, 1.0, 0.0)
            by_sub = by_sub + jnp.where(also, 1.0, 0.0)
        slot_col.append(jnp.sum(by_lane, axis=1, keepdims=True))
        want_buf[g, h:h + 1, :] = own_row[h] * cap + jnp.sum(by_sub, axis=0, keepdims=True)

    block_id = lax.broadcasted_iota(jnp.int32, (blocks, LANES), 0).astype(f32)
    chooser = jnp.concatenate(
        [jnp.where(own_row[h] == block_id, 1.0, 0.0).astype(bf16) for h in range(halves)], axis=1
    )
    base = (d * cap).astype(f32)
    for r in range(groups):
        high, low = [], []
        for h in range(halves):
            at_slot = slot_col[h] == lane + (r * LANES) - base
            local = id_col[h] - own_col[h] * rows
            hi = jnp.floor(local * (1.0 / 256.0))
            high.append(jnp.where(at_slot, hi, 0.0).astype(bf16))
            low.append(jnp.where(at_slot, local - hi * 256.0 + 1.0, 0.0).astype(bf16))
        ask = jnp.dot(chooser, jnp.concatenate(high, axis=0), preferred_element_type=f32) * 256.0
        ask = ask + jnp.dot(chooser, jnp.concatenate(low, axis=0), preferred_element_type=f32)
        req_send[:, :, r * LANES:(r + 1) * LANES] = ask.reshape(n_dev, n_grp, LANES)

    def req_copy(j):
        return pltpu.make_async_remote_copy(
            src_ref=req_send.at[dev_at(j)], dst_ref=req_buf.at[d],
            send_sem=req_ss.at[j], recv_sem=req_rs.at[j], **to_dev(j),
        )

    def start_req(j, carry):
        req_copy(j).start()
        return carry
    lax.fori_loop(1, n_dev, start_req, 0)

    def want_copy(i):
        return pltpu.make_async_remote_copy(
            src_ref=want_buf.at[g], dst_ref=want_buf.at[g],
            send_sem=want_ss.at[i], recv_sem=want_rs.at[i], **to_grp(i),
        )

    for i in range(1, n_grp):
        want_copy(i).start()

    for l in range(layer_share):
        own_copy(l).start()

    req_buf[d] = req_send[d]

    def take_req(j, carry):
        req_copy(j).wait_recv()
        return carry
    lax.fori_loop(1, n_dev, take_req, 0)
    total = req_buf[0]
    for a in range(1, n_dev):
        total = total + req_buf[a]
    for b in range(n_grp):
        merged[g, b] = total[b:b + 1, :]

    def mrg_copy(i):
        return pltpu.make_async_remote_copy(
            src_ref=merged.at[g], dst_ref=merged.at[g],
            send_sem=mrg_ss.at[i], recv_sem=mrg_rs.at[i], **to_grp(i),
        )

    for i in range(n_grp - 1, 0, -1):
        mrg_copy(i).start()
    load_table.wait()

    def z_copy(o, j):
        dp = dev_at(j)
        gp = grp_at(o)
        return pltpu.make_async_remote_copy(
            src_ref=send.at[o, dp],
            dst_ref=recv.at[gp, pl.ds(pl.multiple_of(d * slots, slots), slots), :],
            send_sem=z_ss.at[o, j], recv_sem=z_rs.at[o, j], **to_dev(j),
        )

    spread = LANES // cap
    for o in order:
        gp = grp_at(o)
        if o:
            mrg_copy(back(o)).wait_recv()

        def block(b, carry, o=o, gp=gp):
            at = pl.multiple_of(b * cap, cap)
            for r in range(groups):
                wanted = column(merged[gp, b, :, r * LANES:(r + 1) * LANES]) - (lane + 1.0)
                hit = jnp.concatenate(
                    [(wanted == float(c * LANES)).astype(f32) for c in range(rows // LANES)], axis=1
                ).astype(bf16)
                for l in range(layer_share):
                    found = jnp.dot(
                        hit, tbl[l, pl.ds(pl.multiple_of(b * rows, rows), rows), :],
                        preferred_element_type=f32,
                    ).astype(bf16)
                    send[o, r * spread:(r + 1) * spread, pl.ds(at, cap), l * width:(l + 1) * width] = (
                        found.reshape(spread, cap, width)
                    )
            return carry
        lax.fori_loop(0, n_grp, block, 0)

        def start_z(j, carry, o=o):
            z_copy(o, j).start()
            return carry
        lax.fori_loop(1, n_dev, start_z, 0)
        recv[gp, pl.ds(pl.multiple_of(d * slots, slots), slots), :] = send[o, d]

    load_w.wait()
    load_hidden.wait()
    load_gain.wait()

    def project(l):
        proj = jnp.dot(hidden_ref[...], wbuf[:, l * width:(l + 1) * width], preferred_element_type=f32)
        mean_sq = jnp.mean(proj * proj, axis=-1, keepdims=True)
        return proj / jnp.sqrt(mean_sq + 1e-06) * gain_ref[...]

    for l in range(layers):
        mix[:, l, :] = project(l)

    def e_copy(o):
        return pltpu.make_async_remote_copy(
            src_ref=esend.at[o], dst_ref=erecv.at[g],
            send_sem=e_ss.at[o], recv_sem=e_rs.at[o], **to_grp(o),
        )

    for step, o in enumerate(order):
        gp = grp_at(o)
        if o:
            want_copy(back(o)).wait_recv()
        pickers = []
        for t in range(halves):
            mine = column(want_buf[gp, t:t + 1, :]) - lane
            pickers.append(jnp.concatenate(
                [(mine == float(c * LANES)).astype(f32) for c in range(all_slots // LANES)], axis=1
            ).astype(bf16))

        def take_rows(j, carry, o=o):
            z_copy(o, j).wait_recv()
            return carry
        lax.fori_loop(1, n_dev, take_rows, 0)

        for t in range(halves):
            picked = jnp.dot(pickers[t], recv[gp], preferred_element_type=f32).astype(bf16)
            if o:
                esend[o, t * LANES:(t + 1) * LANES, :] = picked
            else:
                erecv[g, t * LANES:(t + 1) * LANES, :] = picked
        if o:
            e_copy(o).start()
        if step < len(SPLIT):
            start_pieces(step + 1)

    for o in range(1, n_grp):
        e_copy(o).wait_recv()

    for l in range(layers):
        at = (l % layer_share) * width
        emb = erecv[l // layer_share, :, at:at + width].astype(f32)
        mix[:, l, :] = (mix[:, l, :] + math.sqrt(width) * emb) / math.sqrt(2.0)
    out_ref[...] = mix[...].astype(bf16)

    for l in range(layer_share):
        own_copy(l).wait()
    for i in range(1, n_grp):
        want_copy(i).wait_send()
        mrg_copy(i).wait_send()
        e_copy(i).wait_send()

    def end_dev(j, carry):
        req_copy(j).wait_send()
        for o in range(n_grp):
            z_copy(o, j).wait_send()
        return carry
    lax.fori_loop(1, n_dev, end_dev, 0)
    for l, p in pieces:
        for i in range(1, n_grp):
            tab_copy(i, l, p).wait()


def put_out(served_ref, mixed_ref, served_hbm, mixed_hbm, sems):
    parts = sems.shape[0] - 1
    span = served_ref.shape[0] // parts
    copies = [
        pltpu.make_async_copy(
            served_ref.at[pl.ds(k * span, span), :], served_hbm.at[pl.ds(k * span, span), :], sems.at[k]
        )
        for k in range(parts)
    ]
    copies.append(pltpu.make_async_copy(mixed_ref, mixed_hbm, sems.at[parts]))
    for copy in copies:
        copy.start()
    for copy in copies:
        copy.wait()


def on_device(table, token_ids, hidden, w_proj, norm_gain):
    n_grp = lax.axis_size("grp")
    n_dev = lax.axis_size("dev")
    layer_share, vocab_share, width = table.shape
    layers = layer_share * n_grp
    tok = token_ids.shape[0]
    rows = vocab_share // n_grp
    blocks = n_grp * n_dev
    cap = -(-max(2, 2 * tok // blocks) // 16) * 16
    slots = n_grp * cap
    lanes = n_dev * cap
    assert n_grp % 2 == 0 and lanes % LANES == 0 and tok % LANES == 0 and rows % LANES == 0
    wide = layer_share * width

    vmem = pl.BlockSpec(memory_space=pltpu.VMEM)
    hbm = pl.BlockSpec(memory_space=pltpu.HBM)
    dma = pltpu.SemaphoreType.DMA
    bf16 = jnp.bfloat16
    f32 = jnp.float32
    served, mixed = pl.pallas_call(
        functools.partial(exchange, n_grp, n_dev, cap),
        out_shape=(
            pltpu.VMEM((rows, layers * width), bf16),
            pltpu.VMEM((tok, layers, width), bf16),
        ),
        in_specs=[hbm] * 5,
        out_specs=(vmem, vmem),
        scratch_shapes=[
            pltpu.VMEM((tok // LANES, LANES), jnp.int32),
            pltpu.VMEM(hidden.shape, bf16),
            pltpu.VMEM((1, width), f32),
            pltpu.VMEM(table.shape, bf16),
            pltpu.VMEM(w_proj.shape, bf16),
            pltpu.VMEM((n_grp, tok // LANES, LANES), f32),
            pltpu.VMEM((n_dev, n_grp, lanes), f32),
            pltpu.VMEM((n_dev, n_grp, lanes), f32),
            pltpu.VMEM((n_grp, n_grp, 1, lanes), f32),
            pltpu.VMEM((n_grp, n_dev, slots, wide), bf16),
            pltpu.VMEM((n_grp, n_dev * slots, wide), bf16),
            pltpu.VMEM((n_grp, tok, wide), bf16),
            pltpu.VMEM((n_grp, tok, wide), bf16),
            pltpu.VMEM((tok, layers, width), f32),
            dma((n_grp,)), dma((n_grp,)),
            dma((n_dev,)), dma((n_dev,)),
            dma((n_grp,)), dma((n_grp,)),
            dma((n_grp, layer_share, PIECES)), dma((n_grp, layer_share, PIECES)),
            dma((n_grp, n_dev)), dma((n_grp, n_dev)),
            dma((n_grp,)), dma((n_grp,)),
            dma, dma, dma, dma, dma, dma((layer_share,)),
        ],
        compiler_params=pltpu.CompilerParams(
            collective_id=0, has_side_effects=True, vmem_limit_bytes=58 * 2**20
        ),
        name="exchange",
    )(token_ids.reshape(tok // LANES, LANES), hidden, norm_gain.reshape(1, width), table, w_proj)
    served, mixed = pl.pallas_call(
        put_out,
        out_shape=(
            jax.ShapeDtypeStruct(served.shape, bf16),
            jax.ShapeDtypeStruct(mixed.shape, bf16),
        ),
        in_specs=[vmem, vmem],
        out_specs=(hbm, hbm),
        scratch_shapes=[dma((9,))],
        compiler_params=pltpu.CompilerParams(vmem_limit_bytes=2 * 2**20),
        name="put_out",
    )(served, mixed)
    return (served.reshape(1, 1, rows, layers * width), mixed)


def solution(mesh):
    in_specs = (P("grp", "dev", None), P(("grp", "dev")), P(("grp", "dev"), None), P(), P())
    out_specs = (P("dev", "grp", None, None), P(("grp", "dev"), None, None))
    return jax.shard_map(
        on_device, mesh=mesh, in_specs=in_specs, out_specs=out_specs, check_vma=False
    )
```

time: 75.2 us -> 94.8 us (1.26); the launches traced: 73.8 us -> 94.6 us
  Pallas kernels: 67.1 us -> 94 us
  local copies, waits for them, and re-layouts: 5.07 us -> 0 us
  other arithmetic: 1.03 us -> 0 us
    pallas_call x1, Pallas kernels: 67.1 us -> 91.6 us  [on_device(): pl.pallas_call(functools.partial(exchange, n_grp, n_dev, cap), out_shape=...]
    unnamed x6 -> x0, local copies, waits for them, and re-layouts: 4.98 us -> none
    pallas_call x0 -> x1, Pallas kernels: none -> 2.43 us  [on_device(): pl.pallas_call(put_out, out_shape=(jax.ShapeDtypeStruct(served.shape, bf1...]
where the time goes in v1:
time: 94.8 us; the launch traced here: 94.6 us
  Pallas kernels  94 us (99%)
    pallas_call x1, Pallas kernels, on_device(): pl.pallas_call(functools.partial(exchange, n_grp, n_dev, cap), out_shape=...  91.6 us
    pallas_call x1, Pallas kernels, on_device(): pl.pallas_call(put_out, out_shape=(jax.ShapeDtypeStruct(served.shape, bf1...  2.43 us

profile of v1, /device:TPU:25, one launch (start us, length us, event | category | flops | bytes accessed | tf_op | source)
XLA Modules:
  0.0 94.6 jit_solution(464589206247936607)
XLA Ops:
  0.6 91.6 %exchange.1 = (bf16[1024,2048]{1,0:T(8,128)(2,1)S(1)}, bf16[256,8,256]{2,1,0:T(8,128)(2,1)S(1)}) custom-call(s32[2,128]{1,0:T(2,128)} %bitcast.3, bf16[256,2560]{1,0:T(8,128)(2,1)} %hidden_hbm.1, f32[1,256]{1,0:T(1,128)} %bitcast.4, bf16[2,4096,256]{2,1,0:T(8,128)(2,1)} %table_ref.1, bf16[2560,2048]{1,0:T(8,128)(2,1)} %w_ref.1), custom_call_target="tpu_custom_call" | custom-call | tf_op jit(solution)/shard_map/exchange/pallas_call | solution.py:345
  92.2 2.4 %put_out.1 = (bf16[1024,2048]{1,0:T(8,128)(2,1)}, bf16[256,8,256]{2,1,0:T(8,128)(2,1)}) custom-call(bf16[1024,2048]{1,0:T(8,128)(2,1)S(1)} %get-tuple-element.6.served_ref, bf16[256,8,256]{2,1,0:T(8,128)(2,1)S(1)} %get-tuple-element.7.mixed_ref), custom_call_target="tpu_custom_call" | custom-call | tf_op jit(solution)/shard_map/put_out/pallas_call | solution.py:381

commit v2 on v1

v2 whole, which is shorter than its diff:
```python
import functools
import math

import jax
import jax.numpy as jnp
from jax import lax
from jax.experimental import pallas as pl
from jax.experimental.pallas import tpu as pltpu
from jax.sharding import PartitionSpec as P

MESH = pl.DeviceIdType.MESH
LANES = 128
PIECES = 8
SPLIT = (11, 13, 15)
OWN_FIRST = 1


def column(row):
    return jnp.transpose(jnp.broadcast_to(row, (LANES, LANES)))


def exchange(n_grp, n_dev, cap,
             ids_hbm, hidden_hbm, gain_hbm, table_ref, w_ref,
             served_ref, out_ref,
             ids_buf, hidden_ref, gain_ref, tbl, wbuf, want, req_own, req_oth, buf_own, buf_oth, merged,
             send, recv, esend, erecv, mix,
             ids_ss, ids_rs, req_ss, req_rs, tab_ss, tab_rs, z_ss, z_rs, e_ss, e_rs,
             in_grp, in_dev, ids_sem, tbl_sem, w_sem, hidden_sem, gain_sem, own_sem):
    g = lax.axis_index("grp")
    d = lax.axis_index("dev")
    layer_share, vocab_share, width = table_ref.shape
    rows = vocab_share // n_grp
    tok = hidden_ref.shape[0]
    halves = tok // LANES
    layers = layer_share * n_grp
    blocks = n_grp * n_dev
    slots = n_grp * cap
    all_slots = n_dev * slots
    groups = n_dev * cap // LANES
    half_grp = n_grp // 2
    req_send = (req_own, req_oth)
    req_buf = (buf_own, buf_oth)
    f32 = jnp.float32
    bf16 = jnp.bfloat16

    def grp_at(i):
        return lax.rem(g // 2 + i // 2, half_grp) * 2 + lax.rem(g % 2 + i % 2, 2)

    def back(i):
        return ((half_grp - i // 2) % half_grp) * 2 + i % 2

    def dev_at(j):
        return lax.rem(d + j, n_dev)

    def to_grp(i):
        return dict(device_id={"grp": grp_at(i), "dev": d}, device_id_type=MESH)

    def to_dev(j):
        return dict(device_id={"grp": g, "dev": dev_at(j)}, device_id_type=MESH)

    barrier = pltpu.get_barrier_semaphore()
    for i in range(1, n_grp):
        @pl.when(grp_at(i) > g)
        def _(i=i):
            pl.semaphore_signal(barrier, inc=1, **to_grp(i))

    def greet(j, carry):
        pl.semaphore_signal(barrier, inc=1, **to_dev(j))
        return carry
    lax.fori_loop(1, n_dev - d, greet, 0)

    load_ids = pltpu.make_async_copy(ids_hbm, ids_buf.at[g], ids_sem)
    load_ids.start()
    load_table = pltpu.make_async_copy(table_ref, tbl, tbl_sem)
    load_table.start()
    load_w = pltpu.make_async_copy(w_ref, wbuf, w_sem)
    load_w.start()
    load_hidden = pltpu.make_async_copy(hidden_hbm, hidden_ref, hidden_sem)
    load_hidden.start()
    load_gain = pltpu.make_async_copy(gain_hbm, gain_ref, gain_sem)
    load_gain.start()

    part = rows // PIECES
    pieces = [(l, p) for l in range(layer_share) for p in range(PIECES)]

    def tab_copy(i, l, p):
        gp = grp_at(i)
        return pltpu.make_async_remote_copy(
            src_ref=table_ref.at[l, pl.ds(pl.multiple_of(gp * rows + p * part, part), part), :],
            dst_ref=served_ref.at[
                pl.ds(p * part, part),
                pl.ds(pl.multiple_of((g * layer_share + l) * width, width), width),
            ],
            send_sem=tab_ss.at[i, l, p], recv_sem=tab_rs.at[i, l, p], **to_grp(i),
        )

    cuts = [1] + [len(pieces) * s // 16 for s in SPLIT] + [len(pieces)]

    def start_pieces(k):
        for l, p in pieces[cuts[k]:cuts[k + 1]] if k <= len(SPLIT) else ():
            for i in range(n_grp - 1, 0, -1):
                tab_copy(i, l, p).start()

    def own_copy(l):
        return pltpu.make_async_copy(
            table_ref.at[l, pl.ds(pl.multiple_of(g * rows, rows), rows), :],
            served_ref.at[:, pl.ds(pl.multiple_of((g * layer_share + l) * width, width), width)],
            own_sem.at[l],
        )

    def ids_copy(i):
        return pltpu.make_async_remote_copy(
            src_ref=ids_buf.at[g], dst_ref=ids_buf.at[g],
            send_sem=ids_ss.at[i], recv_sem=ids_rs.at[i], **to_grp(i),
        )

    @pl.when(g + d > 0)
    def _():
        pl.semaphore_wait(barrier, g + d)
    for i in range(1, n_grp):
        @pl.when(grp_at(i) < g)
        def _(i=i):
            pl.semaphore_signal(in_grp.at[back(i)], inc=1, **to_grp(i))

    def reply(j, carry):
        pl.semaphore_signal(in_dev, inc=1, **to_dev(j))
        return carry
    lax.fori_loop(n_dev - d, n_dev, reply, 0)

    load_ids.wait()
    for i in range(1, n_grp):
        @pl.when(grp_at(i) > g)
        def _(i=i):
            pl.semaphore_wait(in_grp.at[i], 1)
        ids_copy(i).start()
        l, p = pieces[0]
        tab_copy(i, l, p).start()
    start_pieces(0)
    for l in range(layer_share):
        own_copy(l).start()

    lane = lax.broadcasted_iota(jnp.int32, (LANES, LANES), 1).astype(f32)
    sub = lax.broadcasted_iota(jnp.int32, (LANES, LANES), 0).astype(f32)
    block_id = lax.broadcasted_iota(jnp.int32, (blocks, LANES), 0).astype(f32)
    base = (d * cap).astype(f32)

    def owner_of(v):
        return jnp.floor((v + 0.5) * (1.0 / rows))

    def ask_for(o, req, row):
        gp = grp_at(o)
        id_row = [ids_buf[gp, h:h + 1, :].astype(f32) for h in range(halves)]
        id_col = [column(v) for v in id_row]
        own_row = [owner_of(v) for v in id_row]
        own_col = [owner_of(v) for v in id_col]
        slot_col = []
        for h in range(halves):
            earlier = jnp.zeros((LANES, LANES), f32)
            for k in range(h + 1):
                same = own_col[h] == own_row[k]
                if k == h:
                    same = same & (lane < sub)
                earlier = earlier + jnp.where(same, 1.0, 0.0)
            slot_col.append(jnp.sum(earlier, axis=1, keepdims=True))
            want[o, h] = own_col[h] * cap + slot_col[h]
        chooser = jnp.concatenate(
            [jnp.where(own_row[h] == block_id, 1.0, 0.0).astype(bf16) for h in range(halves)], axis=1
        )
        for r in range(groups):
            high, low = [], []
            for h in range(halves):
                at_slot = slot_col[h] == lane + (r * LANES) - base
                local = id_col[h] - own_col[h] * rows
                hi = jnp.floor(local * (1.0 / 256.0))
                high.append(jnp.where(at_slot, hi, 0.0).astype(bf16))
                low.append(jnp.where(at_slot, local - hi * 256.0 + 1.0, 0.0).astype(bf16))
            ask = jnp.dot(chooser, jnp.concatenate(high, axis=0), preferred_element_type=f32) * 256.0
            ask = ask + jnp.dot(chooser, jnp.concatenate(low, axis=0), preferred_element_type=f32)
            req[:, row:row + n_grp, r * LANES:(r + 1) * LANES] = (
                ask.reshape(n_dev, n_grp, LANES)
            )

    def req_copy(k, j):
        return pltpu.make_async_remote_copy(
            src_ref=req_send[k].at[dev_at(j)], dst_ref=req_buf[k].at[d],
            send_sem=req_ss.at[k, j], recv_sem=req_rs.at[k, j], **to_dev(j),
        )

    def start_req(k):
        def body(j, carry):
            req_copy(k, j).start()
            return carry
        lax.fori_loop(1, n_dev, body, 0)
        req_buf[k][d] = req_send[k][d]

    def take_req(k):
        def body(j, carry):
            req_copy(k, j).wait_recv()
            return carry
        lax.fori_loop(1, n_dev, body, 0)
        total = req_buf[k][0]
        for a in range(1, n_dev):
            total = total + req_buf[k][a]
        return total

    ask_for(0, req_send[0], 0)
    @pl.when(d < n_dev - 1)
    def _():
        pl.semaphore_wait(in_dev, n_dev - 1 - d)
    start_req(0)
    for o in range(1, n_grp):
        ids_copy(back(o)).wait_recv()
    for o in range(1, n_grp):
        ask_for(o, req_send[1], (o - 1) * n_grp)
    start_req(1)

    first = max(1, n_grp * OWN_FIRST // 4)
    phases = [(0, 0, first)] + [(o, 0, n_grp) for o in range(n_grp - 1, 0, -1)] + [(0, first, n_grp)]

    def z_copy(f, j):
        o, lo, hi = phases[f]
        span = (hi - lo) * cap
        return pltpu.make_async_remote_copy(
            src_ref=send.at[o, dev_at(j), lo * cap:hi * cap],
            dst_ref=recv.at[grp_at(o), pl.ds(pl.multiple_of(d * slots + lo * cap, cap), span), :],
            send_sem=z_ss.at[f, j], recv_sem=z_rs.at[f, j], **to_dev(j),
        )

    spread = LANES // cap
    total = take_req(0)
    for b in range(n_grp):
        merged[0, b] = total[b:b + 1, :]
    load_table.wait()
    for f, (o, lo, hi) in enumerate(phases):
        if f == 1:
            total = take_req(1)
            for k in range(n_grp, n_grp * n_grp):
                merged[k // n_grp, k % n_grp] = total[k - n_grp:k - n_grp + 1, :]

        def block(b, carry, o=o):
            at = pl.multiple_of(b * cap, cap)
            for r in range(groups):
                wanted = column(merged[o, b, :, r * LANES:(r + 1) * LANES]) - (lane + 1.0)
                hit = jnp.concatenate(
                    [(wanted == float(c * LANES)).astype(f32) for c in range(rows // LANES)], axis=1
                ).astype(bf16)
                for l in range(layer_share):
                    found = jnp.dot(
                        hit, tbl[l, pl.ds(pl.multiple_of(b * rows, rows), rows), :],
                        preferred_element_type=f32,
                    ).astype(bf16)
                    send[o, r * spread:(r + 1) * spread, pl.ds(at, cap), l * width:(l + 1) * width] = (
                        found.reshape(spread, cap, width)
                    )
            return carry
        lax.fori_loop(lo, hi, block, 0)

        def start_z(j, carry, f=f):
            z_copy(f, j).start()
            return carry
        lax.fori_loop(1, n_dev, start_z, 0)
        recv[grp_at(o), pl.ds(pl.multiple_of(d * slots + lo * cap, cap), (hi - lo) * cap), :] = (
            send[o, d, lo * cap:hi * cap]
        )

    load_w.wait()
    load_hidden.wait()
    load_gain.wait()

    def project(l):
        proj = jnp.dot(hidden_ref[...], wbuf[:, l * width:(l + 1) * width], preferred_element_type=f32)
        mean_sq = jnp.mean(proj * proj, axis=-1, keepdims=True)
        return proj / jnp.sqrt(mean_sq + 1e-06) * gain_ref[...]

    for l in range(layers):
        mix[:, l, :] = project(l)

    def e_copy(o):
        return pltpu.make_async_remote_copy(
            src_ref=esend.at[o], dst_ref=erecv.at[g],
            send_sem=e_ss.at[o], recv_sem=e_rs.at[o], **to_grp(o),
        )

    def take_rows(f):
        def body(j, carry):
            z_copy(f, j).wait_recv()
            return carry
        lax.fori_loop(1, n_dev, body, 0)

    def pickers(o):
        made = []
        for t in range(halves):
            mine = want[o, t] - lane
            made.append(jnp.concatenate(
                [(mine == float(c * LANES)).astype(f32) for c in range(all_slots // LANES)], axis=1
            ).astype(bf16))
        return made

    def pick(o, dst, at):
        for t, picker in enumerate(pickers(o)):
            dst[at, t * LANES:(t + 1) * LANES, :] = jnp.dot(
                picker, recv[grp_at(o)], preferred_element_type=f32
            ).astype(bf16)

    def add_rows(a):
        for k in range(layer_share):
            l = a * layer_share + k
            emb = erecv[a, :, k * width:(k + 1) * width].astype(f32)
            mix[:, l, :] = (mix[:, l, :] + math.sqrt(width) * emb) / math.sqrt(2.0)

    for f in range(1, n_grp):
        take_rows(f)
        pick(phases[f][0], esend, phases[f][0])
        e_copy(phases[f][0]).start()
        start_pieces(f)

    for o in range(1, n_grp):
        e_copy(o).wait_recv()
    for a in range(n_grp):
        @pl.when(g != a)
        def _(a=a):
            add_rows(a)
    take_rows(0)
    take_rows(n_grp)
    pick(0, erecv, g)
    for a in range(n_grp):
        @pl.when(g == a)
        def _(a=a):
            add_rows(a)
    out_ref[...] = mix[...].astype(bf16)

    for l in range(layer_share):
        own_copy(l).wait()
    for i in range(1, n_grp):
        ids_copy(i).wait_send()
        e_copy(i).wait_send()

    def end_dev(j, carry):
        for k in range(2):
            req_copy(k, j).wait_send()
        for f in range(n_grp + 1):
            z_copy(f, j).wait_send()
        return carry
    lax.fori_loop(1, n_dev, end_dev, 0)
    for l, p in pieces:
        for i in range(1, n_grp):
            tab_copy(i, l, p).wait()


def put_out(served_ref, mixed_ref, served_hbm, mixed_hbm, sems):
    parts = sems.shape[0] - 1
    span = served_ref.shape[0] // parts
    copies = [
        pltpu.make_async_copy(
            served_ref.at[pl.ds(k * span, span), :], served_hbm.at[pl.ds(k * span, span), :], sems.at[k]
        )
        for k in range(parts)
    ]
    copies.append(pltpu.make_async_copy(mixed_ref, mixed_hbm, sems.at[parts]))
    for copy in copies:
        copy.start()
    for copy in copies:
        copy.wait()


def on_device(table, token_ids, hidden, w_proj, norm_gain):
    n_grp = lax.axis_size("grp")
    n_dev = lax.axis_size("dev")
    layer_share, vocab_share, width = table.shape
    layers = layer_share * n_grp
    tok = token_ids.shape[0]
    rows = vocab_share // n_grp
    blocks = n_grp * n_dev
    cap = -(-max(2, 2 * tok // blocks) // 16) * 16
    slots = n_grp * cap
    lanes = n_dev * cap
    assert n_grp % 2 == 0 and lanes % LANES == 0 and tok % LANES == 0 and rows % LANES == 0
    wide = layer_share * width

    vmem = pl.BlockSpec(memory_space=pltpu.VMEM)
    hbm = pl.BlockSpec(memory_space=pltpu.HBM)
    dma = pltpu.SemaphoreType.DMA
    bf16 = jnp.bfloat16
    f32 = jnp.float32
    served, mixed = pl.pallas_call(
        functools.partial(exchange, n_grp, n_dev, cap),
        out_shape=(
            pltpu.VMEM((rows, layers * width), bf16),
            pltpu.VMEM((tok, layers, width), bf16),
        ),
        in_specs=[hbm] * 5,
        out_specs=(vmem, vmem),
        scratch_shapes=[
            pltpu.VMEM((n_grp, tok // LANES, LANES), jnp.int32),
            pltpu.VMEM(hidden.shape, bf16),
            pltpu.VMEM((1, width), f32),
            pltpu.VMEM(table.shape, bf16),
            pltpu.VMEM(w_proj.shape, bf16),
            pltpu.VMEM((n_grp, tok // LANES, LANES, LANES), f32),
            pltpu.VMEM((n_dev, n_grp, lanes), f32),
            pltpu.VMEM((n_dev, (n_grp - 1) * n_grp, lanes), f32),
            pltpu.VMEM((n_dev, n_grp, lanes), f32),
            pltpu.VMEM((n_dev, (n_grp - 1) * n_grp, lanes), f32),
            pltpu.VMEM((n_grp, n_grp, 1, lanes), f32),
            pltpu.VMEM((n_grp, n_dev, slots, wide), bf16),
            pltpu.VMEM((n_grp, n_dev * slots, wide), bf16),
            pltpu.VMEM((n_grp, tok, wide), bf16),
            pltpu.VMEM((n_grp, tok, wide), bf16),
            pltpu.VMEM((tok, layers, width), f32),
            dma((n_grp,)), dma((n_grp,)),
            dma((2, n_dev)), dma((2, n_dev)),
            dma((n_grp, layer_share, PIECES)), dma((n_grp, layer_share, PIECES)),
            dma((n_grp + 1, n_dev)), dma((n_grp + 1, n_dev)),
            dma((n_grp,)), dma((n_grp,)),
            pltpu.SemaphoreType.REGULAR((n_grp,)), pltpu.SemaphoreType.REGULAR,
            dma, dma, dma, dma, dma, dma((layer_share,)),
        ],
        compiler_params=pltpu.CompilerParams(
            collective_id=0, has_side_effects=True, vmem_limit_bytes=58 * 2**20
        ),
        name="exchange",
    )(token_ids.reshape(tok // LANES, LANES), hidden, norm_gain.reshape(1, width), table, w_proj)
    served, mixed = pl.pallas_call(
        put_out,
        out_shape=(
            jax.ShapeDtypeStruct(served.shape, bf16),
            jax.ShapeDtypeStruct(mixed.shape, bf16),
        ),
        in_specs=[vmem, vmem],
        out_specs=(hbm, hbm),
        scratch_shapes=[dma((9,))],
        compiler_params=pltpu.CompilerParams(vmem_limit_bytes=2 * 2**20),
        name="put_out",
    )(served, mixed)
    return (served.reshape(1, 1, rows, layers * width), mixed)


def solution(mesh):
    in_specs = (P("grp", "dev", None), P(("grp", "dev")), P(("grp", "dev"), None), P(), P())
    out_specs = (P("dev", "grp", None, None), P(("grp", "dev"), None, None))
    return jax.shard_map(
        on_device, mesh=mesh, in_specs=in_specs, out_specs=out_specs, check_vma=False
    )
```

time: 94.8 us -> 69.2 us (0.73)
  Pallas kernels: 94 us -> 68.4 us
    pallas_call x1, Pallas kernels: 91.6 us -> 65.9 us  [on_device(): pl.pallas_call(functools.partial(exchange, n_grp, n_dev, cap), out_shape=...]
where the time goes in v2:
time: 69.2 us; the launch traced here: 69 us
  Pallas kernels  68.4 us (99%)
    pallas_call x1, Pallas kernels, on_device(): pl.pallas_call(functools.partial(exchange, n_grp, n_dev, cap), out_shape=...  65.9 us
    pallas_call x1, Pallas kernels, on_device(): pl.pallas_call(put_out, out_shape=(jax.ShapeDtypeStruct(served.shape, bf1...  2.43 us

profile of v2, /device:TPU:25, one launch (start us, length us, event | category | flops | bytes accessed | tf_op | source)
XLA Modules:
  0.0 69.0 jit_solution(11940759574248397491)
XLA Ops:
  0.6 65.9 %exchange.1 = (bf16[1024,2048]{1,0:T(8,128)(2,1)S(1)}, bf16[256,8,256]{2,1,0:T(8,128)(2,1)S(1)}) custom-call(s32[2,128]{1,0:T(2,128)} %bitcast.3, bf16[256,2560]{1,0:T(8,128)(2,1)} %hidden_hbm.1, f32[1,256]{1,0:T(1,128)} %bitcast.4, bf16[2,4096,256]{2,1,0:T(8,128)(2,1)} %table_ref.1, bf16[2560,2048]{1,0:T(8,128)(2,1)} %w_ref.1), custom_call_target="tpu_custom_call" | custom-call | tf_op jit(solution)/shard_map/exchange/pallas_call | solution.py:385
  66.6 2.4 %put_out.1 = (bf16[1024,2048]{1,0:T(8,128)(2,1)}, bf16[256,8,256]{2,1,0:T(8,128)(2,1)}) custom-call(bf16[1024,2048]{1,0:T(8,128)(2,1)S(1)} %get-tuple-element.6.served_ref, bf16[256,8,256]{2,1,0:T(8,128)(2,1)S(1)} %get-tuple-element.7.mixed_ref), custom_call_target="tpu_custom_call" | custom-call | tf_op jit(solution)/shard_map/put_out/pallas_call | solution.py:423

commit v3 on v2

--- a/solution.py
+++ b/solution.py
@@ -11,8 +11,9 @@
 MESH = pl.DeviceIdType.MESH
 LANES = 128
 PIECES = 8
-SPLIT = (11, 13, 15)
+SPLIT = (12, 14, 15)
 OWN_FIRST = 1
+AHEAD = 2
 
 
 def column(row):
@@ -58,6 +59,9 @@
     def to_dev(j):
         return dict(device_id={"grp": g, "dev": dev_at(j)}, device_id_type=MESH)
 
+    def drain(part, sem):
+        pltpu.make_async_copy(part, part, sem).wait()
+
     barrier = pltpu.get_barrier_semaphore()
     for i in range(1, n_grp):
         @pl.when(grp_at(i) > g)
@@ -72,13 +76,9 @@
     load_ids = pltpu.make_async_copy(ids_hbm, ids_buf.at[g], ids_sem)
     load_ids.start()
     load_table = pltpu.make_async_copy(table_ref, tbl, tbl_sem)
-    load_table.start()
     load_w = pltpu.make_async_copy(w_ref, wbuf, w_sem)
-    load_w.start()
     load_hidden = pltpu.make_async_copy(hidden_hbm, hidden_ref, hidden_sem)
-    load_hidden.start()
     load_gain = pltpu.make_async_copy(gain_hbm, gain_ref, gain_sem)
-    load_gain.start()
 
     part = rows // PIECES
     pieces = [(l, p) for l in range(layer_share) for p in range(PIECES)]
@@ -91,7 +91,7 @@
                 pl.ds(p * part, part),
                 pl.ds(pl.multiple_of((g * layer_share + l) * width, width), width),
             ],
-            send_sem=tab_ss.at[i, l, p], recv_sem=tab_rs.at[i, l, p], **to_grp(i),
+            send_sem=tab_ss, recv_sem=tab_rs, **to_grp(i),
         )
 
     cuts = [1] + [len(pieces) * s // 16 for s in SPLIT] + [len(pieces)]
@@ -105,13 +105,13 @@
         return pltpu.make_async_copy(
             table_ref.at[l, pl.ds(pl.multiple_of(g * rows, rows), rows), :],
             served_ref.at[:, pl.ds(pl.multiple_of((g * layer_share + l) * width, width), width)],
-            own_sem.at[l],
+            own_sem,
         )
 
     def ids_copy(i):
         return pltpu.make_async_remote_copy(
             src_ref=ids_buf.at[g], dst_ref=ids_buf.at[g],
-            send_sem=ids_ss.at[i], recv_sem=ids_rs.at[i], **to_grp(i),
+            send_sem=ids_ss, recv_sem=ids_rs, **to_grp(i),
         )
 
     @pl.when(g + d > 0)
@@ -136,6 +136,7 @@
         l, p = pieces[0]
         tab_copy(i, l, p).start()
     start_pieces(0)
+    load_table.start()
     for l in range(layer_share):
         own_copy(l).start()
 
@@ -183,7 +184,7 @@
     def req_copy(k, j):
         return pltpu.make_async_remote_copy(
             src_ref=req_send[k].at[dev_at(j)], dst_ref=req_buf[k].at[d],
-            send_sem=req_ss.at[k, j], recv_sem=req_rs.at[k, j], **to_dev(j),
+            send_sem=req_ss.at[k], recv_sem=req_rs.at[k], **to_dev(j),
         )
 
     def start_req(k):
@@ -194,74 +195,93 @@
         req_buf[k][d] = req_send[k][d]
 
     def take_req(k):
-        def body(j, carry):
-            req_copy(k, j).wait_recv()
-            return carry
-        lax.fori_loop(1, n_dev, body, 0)
+        drain(req_buf[k].at[pl.ds(0, n_dev - 1)], req_rs.at[k])
         total = req_buf[k][0]
         for a in range(1, n_dev):
             total = total + req_buf[k][a]
         return total
 
+    load_w.start()
+    load_hidden.start()
+    load_gain.start()
     ask_for(0, req_send[0], 0)
     @pl.when(d < n_dev - 1)
     def _():
         pl.semaphore_wait(in_dev, n_dev - 1 - d)
     start_req(0)
-    for o in range(1, n_grp):
-        ids_copy(back(o)).wait_recv()
+    drain(ids_buf.at[pl.ds(0, n_grp - 1)], ids_rs)
     for o in range(1, n_grp):
         ask_for(o, req_send[1], (o - 1) * n_grp)
     start_req(1)
 
     first = max(1, n_grp * OWN_FIRST // 4)
-    phases = [(0, 0, first)] + [(o, 0, n_grp) for o in range(n_grp - 1, 0, -1)] + [(0, first, n_grp)]
-
-    def z_copy(f, j):
-        o, lo, hi = phases[f]
+    wide = layer_share * width
+    both = [o for o in range(n_grp - 1, 0, -1) if o // 2 and o % 2]
+    single = [o for o in range(1, n_grp) if o not in both]
+    units = [(0, 0, first, 0, wide)] + [(o, 0, n_grp, 0, wide) for o in both]
+    steps = [[u] for u in range(len(units))]
+    for c0 in (0, wide // 2):
+        steps.append(list(range(len(units), len(units) + len(single))))
+        units += [(o, 0, n_grp, c0, c0 + wide // 2) for o in single]
+    steps.append([len(units)])
+    units.append((0, first, n_grp, 0, wide))
+    last = len(steps) - 1
+
+    def z_copy(u, j):
+        o, lo, hi, c0, c1 = units[u]
         span = (hi - lo) * cap
         return pltpu.make_async_remote_copy(
-            src_ref=send.at[o, dev_at(j), lo * cap:hi * cap],
-            dst_ref=recv.at[grp_at(o), pl.ds(pl.multiple_of(d * slots + lo * cap, cap), span), :],
-            send_sem=z_ss.at[f, j], recv_sem=z_rs.at[f, j], **to_dev(j),
-        )
+            src_ref=send.at[o, dev_at(j), lo * cap:hi * cap, c0:c1],
+            dst_ref=recv.at[grp_at(o), pl.ds(pl.multiple_of(d * slots + lo * cap, cap), span), c0:c1],
+            send_sem=z_ss, recv_sem=z_rs.at[u], **to_dev(j),
+        )
+
+    def start_rows(s):
+        def body(j, carry):
+            for u in steps[s]:
+                z_copy(u, j).start()
+            return carry
+        lax.fori_loop(1, n_dev, body, 0)
 
     spread = LANES // cap
     total = take_req(0)
     for b in range(n_grp):
         merged[0, b] = total[b:b + 1, :]
     load_table.wait()
-    for f, (o, lo, hi) in enumerate(phases):
+    looked = set()
+    for f, members in enumerate(steps):
         if f == 1:
             total = take_req(1)
             for k in range(n_grp, n_grp * n_grp):
                 merged[k // n_grp, k % n_grp] = total[k - n_grp:k - n_grp + 1, :]
 
-        def block(b, carry, o=o):
-            at = pl.multiple_of(b * cap, cap)
-            for r in range(groups):
-                wanted = column(merged[o, b, :, r * LANES:(r + 1) * LANES]) - (lane + 1.0)
-                hit = jnp.concatenate(
-                    [(wanted == float(c * LANES)).astype(f32) for c in range(rows // LANES)], axis=1
-                ).astype(bf16)
-                for l in range(layer_share):
-                    found = jnp.dot(
-                        hit, tbl[l, pl.ds(pl.multiple_of(b * rows, rows), rows), :],
-                        preferred_element_type=f32,
+        for o, lo, hi in [units[u][:3] for u in members]:
+            if (o, lo) in looked:
+                continue
+            looked.add((o, lo))
+
+            def block(b, carry, o=o):
+                at = pl.multiple_of(b * cap, cap)
+                for r in range(groups):
+                    wanted = column(merged[o, b, :, r * LANES:(r + 1) * LANES]) - (lane + 1.0)
+                    hit = jnp.concatenate(
+                        [(wanted == float(c * LANES)).astype(f32) for c in range(rows // LANES)], axis=1
                     ).astype(bf16)
-                    send[o, r * spread:(r + 1) * spread, pl.ds(at, cap), l * width:(l + 1) * width] = (
-                        found.reshape(spread, cap, width)
-                    )
-            return carry
-        lax.fori_loop(lo, hi, block, 0)
-
-        def start_z(j, carry, f=f):
-            z_copy(f, j).start()
-            return carry
-        lax.fori_loop(1, n_dev, start_z, 0)
-        recv[grp_at(o), pl.ds(pl.multiple_of(d * slots + lo * cap, cap), (hi - lo) * cap), :] = (
-            send[o, d, lo * cap:hi * cap]
-        )
+                    for l in range(layer_share):
+                        found = jnp.dot(
+                            hit, tbl[l, pl.ds(pl.multiple_of(b * rows, rows), rows), :],
+                            preferred_element_type=f32,
+                        ).astype(bf16)
+                        send[o, r * spread:(r + 1) * spread, pl.ds(at, cap), l * width:(l + 1) * width] = (
+                            found.reshape(spread, cap, width)
+                        )
+                return carry
+            lax.fori_loop(lo, hi, block, 0)
+            recv[grp_at(o), pl.ds(pl.multiple_of(d * slots + lo * cap, cap), (hi - lo) * cap), :] = (
+                send[o, d, lo * cap:hi * cap]
+            )
+        if f < AHEAD:
+            start_rows(f)
 
     load_w.wait()
     load_hidden.wait()
@@ -275,17 +295,17 @@
     for l in range(layers):
         mix[:, l, :] = project(l)
 
-    def e_copy(o):
+    def e_copy(u):
+        o, _, _, c0, c1 = units[u]
         return pltpu.make_async_remote_copy(
-            src_ref=esend.at[o], dst_ref=erecv.at[g],
-            send_sem=e_ss.at[o], recv_sem=e_rs.at[o], **to_grp(o),
+            src_ref=esend.at[o, :, c0:c1], dst_ref=erecv.at[g, :, c0:c1],
+            send_sem=e_ss, recv_sem=e_rs.at[u], **to_grp(o),
         )
 
     def take_rows(f):
-        def body(j, carry):
-            z_copy(f, j).wait_recv()
-            return carry
-        lax.fori_loop(1, n_dev, body, 0)
+        for u in steps[f]:
+            o, lo, hi, c0, c1 = units[u]
+            drain(recv.at[0, pl.ds(0, (n_dev - 1) * (hi - lo) * cap), c0:c1], z_rs.at[u])
 
     def pickers(o):
         made = []
@@ -296,55 +316,59 @@
             ).astype(bf16))
         return made
 
-    def pick(o, dst, at):
+    def pick(u, dst, at):
+        o, _, _, c0, c1 = units[u]
         for t, picker in enumerate(pickers(o)):
-            dst[at, t * LANES:(t + 1) * LANES, :] = jnp.dot(
-                picker, recv[grp_at(o)], preferred_element_type=f32
+            dst[at, t * LANES:(t + 1) * LANES, c0:c1] = jnp.dot(
+                picker, recv[grp_at(o), :, c0:c1], preferred_element_type=f32
             ).astype(bf16)
 
-    def add_rows(a):
-        for k in range(layer_share):
-            l = a * layer_share + k
-            emb = erecv[a, :, k * width:(k + 1) * width].astype(f32)
-            mix[:, l, :] = (mix[:, l, :] + math.sqrt(width) * emb) / math.sqrt(2.0)
-
-    for f in range(1, n_grp):
+    def add_rows(source, u):
+        c0, c1 = units[u][3:]
+        for a in range(n_grp):
+            @pl.when(source == a)
+            def _(a=a):
+                for k in range(layer_share):
+                    lo, hi = max(c0, k * width), min(c1, (k + 1) * width)
+                    if lo < hi:
+                        l, at = a * layer_share + k, slice(lo - k * width, hi - k * width)
+                        emb = erecv[a, :, lo:hi].astype(f32)
+                        mix[:, l, at] = (mix[:, l, at] + math.sqrt(width) * emb) / math.sqrt(2.0)
+
+    def add_from_peer(u):
+        e_copy(u).wait_recv()
+        add_rows(grp_at(back(units[u][0])), u)
+
+    take_rows(0)
+    if AHEAD <= last:
+        start_rows(AHEAD)
+    for f in range(1, last):
         take_rows(f)
-        pick(phases[f][0], esend, phases[f][0])
-        e_copy(phases[f][0]).start()
+        if f + AHEAD <= last:
+            start_rows(f + AHEAD)
+        for u in steps[f]:
+            pick(u, esend, units[u][0])
+            e_copy(u).start()
         start_pieces(f)
 
-    for o in range(1, n_grp):
-        e_copy(o).wait_recv()
-    for a in range(n_grp):
-        @pl.when(g != a)
-        def _(a=a):
-            add_rows(a)
-    take_rows(0)
-    take_rows(n_grp)
-    pick(0, erecv, g)
-    for a in range(n_grp):
-        @pl.when(g == a)
-        def _(a=a):
-            add_rows(a)
+    for f in range(1, last - 1):
+        for u in steps[f]:
+            add_from_peer(u)
+    take_rows(last)
+    pick(steps[last][0], erecv, g)
+    add_rows(g, steps[last][0])
+    for u in steps[last - 1]:
+        add_from_peer(u)
     out_ref[...] = mix[...].astype(bf16)
 
-    for l in range(layer_share):
-        own_copy(l).wait()
-    for i in range(1, n_grp):
-        ids_copy(i).wait_send()
-        e_copy(i).wait_send()
-
-    def end_dev(j, carry):
-        for k in range(2):
-            req_copy(k, j).wait_send()
-        for f in range(n_grp + 1):
-            z_copy(f, j).wait_send()
-        return carry
-    lax.fori_loop(1, n_dev, end_dev, 0)
-    for l, p in pieces:
-        for i in range(1, n_grp):
-            tab_copy(i, l, p).wait()
+    drain(served_ref.at[:, pl.ds(0, wide)], own_sem)
+    drain(ids_buf.at[pl.ds(0, n_grp - 1)], ids_ss)
+    for k in range(2):
+        drain(req_send[k].at[pl.ds(0, n_dev - 1)], req_ss.at[k])
+    drain(send.at[:, pl.ds(0, n_dev - 1)], z_ss)
+    drain(esend.at[pl.ds(0, n_grp - 1)], e_ss)
+    drain(served_ref.at[:, pl.ds(0, (n_grp - 1) * wide)], tab_ss)
+    drain(served_ref.at[:, pl.ds(0, (n_grp - 1) * wide)], tab_rs)
 
 
 def put_out(served_ref, mixed_ref, served_hbm, mixed_hbm, sems):
@@ -407,13 +431,13 @@
             pltpu.VMEM((n_grp, tok, wide), bf16),
             pltpu.VMEM((n_grp, tok, wide), bf16),
             pltpu.VMEM((tok, layers, width), f32),
-            dma((n_grp,)), dma((n_grp,)),
-            dma((2, n_dev)), dma((2, n_dev)),
-            dma((n_grp, layer_share, PIECES)), dma((n_grp, layer_share, PIECES)),
-            dma((n_grp + 1, n_dev)), dma((n_grp + 1, n_dev)),
-            dma((n_grp,)), dma((n_grp,)),
+            dma, dma,
+            dma((2,)), dma((2,)),
+            dma, dma,
+            dma, dma((2 * n_grp,)),
+            dma, dma((2 * n_grp,)),
             pltpu.SemaphoreType.REGULAR((n_grp,)), pltpu.SemaphoreType.REGULAR,
-            dma, dma, dma, dma, dma, dma((layer_share,)),
+            dma, dma, dma, dma, dma, dma,
         ],
         compiler_params=pltpu.CompilerParams(
             collective_id=0, has_side_effects=True, vmem_limit_bytes=58 * 2**20

time: 69.2 us -> 65.6 us (0.948)
  the two profiles are of different devices: /device:TPU:25 before, /device:TPU:0 now
where the time goes in v3:
time: 65.6 us; the launch traced here: 65.5 us
  Pallas kernels  64.8 us (99%)
    pallas_call x1, Pallas kernels, on_device(): pl.pallas_call(functools.partial(exchange, n_grp, n_dev, cap), out_shape=...  62.4 us
    pallas_call x1, Pallas kernels, on_device(): pl.pallas_call(put_out, out_shape=(jax.ShapeDtypeStruct(served.shape, bf1...  2.43 us

profile of v3, /device:TPU:0, one launch (start us, length us, event | category | flops | bytes accessed | tf_op | source)
XLA Modules:
  0.0 65.5 jit_solution(11647666802980741736)
XLA Ops:
  0.6 62.4 %exchange.1 = (bf16[1024,2048]{1,0:T(8,128)(2,1)S(1)}, bf16[256,8,256]{2,1,0:T(8,128)(2,1)S(1)}) custom-call(s32[2,128]{1,0:T(2,128)} %bitcast.3, bf16[256,2560]{1,0:T(8,128)(2,1)} %hidden_hbm.1, f32[1,256]{1,0:T(1,128)} %bitcast.4, bf16[2,4096,256]{2,1,0:T(8,128)(2,1)} %table_ref.1, bf16[2560,2048]{1,0:T(8,128)(2,1)} %w_ref.1), custom_call_target="tpu_custom_call" | custom-call | tf_op jit(solution)/shard_map/exchange/pallas_call | solution.py:409
  63.0 2.4 %put_out.1 = (bf16[1024,2048]{1,0:T(8,128)(2,1)}, bf16[256,8,256]{2,1,0:T(8,128)(2,1)}) custom-call(bf16[1024,2048]{1,0:T(8,128)(2,1)S(1)} %get-tuple-element.6.served_ref, bf16[256,8,256]{2,1,0:T(8,128)(2,1)S(1)} %get-tuple-element.7.mixed_ref), custom_call_target="tpu_custom_call" | custom-call | tf_op jit(solution)/shard_map/put_out/pallas_call | solution.py:447

commit v4 on v3

--- a/solution.py
+++ b/solution.py
@@ -62,9 +62,19 @@
     def drain(part, sem):
         pltpu.make_async_copy(part, part, sem).wait()
 
+    high, low = g // 2, g % 2
+
+    def below(i):
+        p = grp_at(i)
+        return (p // 2 <= high) & (p % 2 <= low)
+
+    def above(i):
+        p = grp_at(i)
+        return (p // 2 >= high) & (p % 2 >= low)
+
     barrier = pltpu.get_barrier_semaphore()
     for i in range(1, n_grp):
-        @pl.when(grp_at(i) > g)
+        @pl.when(above(i))
         def _(i=i):
             pl.semaphore_signal(barrier, inc=1, **to_grp(i))
 
@@ -83,12 +93,13 @@
     part = rows // PIECES
     pieces = [(l, p) for l in range(layer_share) for p in range(PIECES)]
 
-    def tab_copy(i, l, p):
+    def tab_copy(i, l, p, at=0, part=part):
         gp = grp_at(i)
+        first_row = p * (rows // PIECES) + at
         return pltpu.make_async_remote_copy(
-            src_ref=table_ref.at[l, pl.ds(pl.multiple_of(gp * rows + p * part, part), part), :],
+            src_ref=table_ref.at[l, pl.ds(pl.multiple_of(gp * rows + first_row, part), part), :],
             dst_ref=served_ref.at[
-                pl.ds(p * part, part),
+                pl.ds(first_row, part),
                 pl.ds(pl.multiple_of((g * layer_share + l) * width, width), width),
             ],
             send_sem=tab_ss, recv_sem=tab_rs, **to_grp(i),
@@ -116,9 +127,9 @@
 
     @pl.when(g + d > 0)
     def _():
-        pl.semaphore_wait(barrier, g + d)
+        pl.semaphore_wait(barrier, (high + 1) * (low + 1) - 1 + d)
     for i in range(1, n_grp):
-        @pl.when(grp_at(i) < g)
+        @pl.when(below(i))
         def _(i=i):
             pl.semaphore_signal(in_grp.at[back(i)], inc=1, **to_grp(i))
 
@@ -127,14 +138,27 @@
         return carry
     lax.fori_loop(n_dev - d, n_dev, reply, 0)
 
+    l, p = pieces[0]
+    half = part // 2
+    for i in range(1, n_grp):
+        @pl.when(below(i))
+        def _(i=i):
+            tab_copy(i, l, p, 0, half).start()
     load_ids.wait()
     for i in range(1, n_grp):
-        @pl.when(grp_at(i) > g)
+        @pl.when(jnp.logical_not(below(i)))
         def _(i=i):
             pl.semaphore_wait(in_grp.at[i], 1)
+        if i % 2 == 0:
+            @pl.when((low == 0) & (high + i // 2 < half_grp))
+            def _(i=i):
+                pl.semaphore_signal(in_grp.at[i + 1], inc=1, **to_grp(1))
+                pl.semaphore_signal(in_grp.at[n_grp - i + 1], inc=1, **to_grp(i))
         ids_copy(i).start()
-        l, p = pieces[0]
-        tab_copy(i, l, p).start()
+        @pl.when(jnp.logical_not(below(i)))
+        def _(i=i):
+            tab_copy(i, l, p, 0, half).start()
+        tab_copy(i, l, p, half, half).start()
     start_pieces(0)
     load_table.start()
     for l in range(layer_share):

time: 65.6 us -> 64.9 us (0.989)
  the two profiles are of different devices: /device:TPU:0 before, /device:TPU:25 now
where the time goes in v4:
time: 64.9 us; the launch traced here: 63.8 us
  Pallas kernels  63.2 us (97%)
    pallas_call x1, Pallas kernels, on_device(): pl.pallas_call(functools.partial(exchange, n_grp, n_dev, cap), out_shape=...  60.8 us
    pallas_call x1, Pallas kernels, on_device(): pl.pallas_call(put_out, out_shape=(jax.ShapeDtypeStruct(served.shape, bf1...  2.43 us

profile of v4, /device:TPU:25, one launch (start us, length us, event | category | flops | bytes accessed | tf_op | source)
XLA Modules:
  0.0 63.8 jit_solution(3912597215708007705)
XLA Ops:
  0.6 60.8 %exchange.1 = (bf16[1024,2048]{1,0:T(8,128)(2,1)S(1)}, bf16[256,8,256]{2,1,0:T(8,128)(2,1)S(1)}) custom-call(s32[2,128]{1,0:T(2,128)} %bitcast.3, bf16[256,2560]{1,0:T(8,128)(2,1)} %hidden_hbm.1, f32[1,256]{1,0:T(1,128)} %bitcast.4, bf16[2,4096,256]{2,1,0:T(8,128)(2,1)} %table_ref.1, bf16[2560,2048]{1,0:T(8,128)(2,1)} %w_ref.1), custom_call_target="tpu_custom_call" | custom-call | tf_op jit(solution)/shard_map/exchange/pallas_call | solution.py:433
  61.4 2.4 %put_out.1 = (bf16[1024,2048]{1,0:T(8,128)(2,1)}, bf16[256,8,256]{2,1,0:T(8,128)(2,1)}) custom-call(bf16[1024,2048]{1,0:T(8,128)(2,1)S(1)} %get-tuple-element.6.served_ref, bf16[256,8,256]{2,1,0:T(8,128)(2,1)S(1)} %get-tuple-element.7.mixed_ref), custom_call_target="tpu_custom_call" | custom-call | tf_op jit(solution)/shard_map/put_out/pallas_call | solution.py:471

commit v5 on v4

--- a/solution.py
+++ b/solution.py
@@ -11,7 +11,7 @@
 MESH = pl.DeviceIdType.MESH
 LANES = 128
 PIECES = 8
-SPLIT = (12, 14, 15)
+SPLIT = (13, 14, 15)
 OWN_FIRST = 1
 AHEAD = 2
 

time: 64.9 us -> 64.9 us (level)
  no operation moved by 1% of the time
where the time goes in v5:
time: 64.9 us; the launch traced here: 63.8 us
  Pallas kernels  63.2 us (97%)
    pallas_call x1, Pallas kernels, on_device(): pl.pallas_call(functools.partial(exchange, n_grp, n_dev, cap), out_shape=...  60.8 us
    pallas_call x1, Pallas kernels, on_device(): pl.pallas_call(put_out, out_shape=(jax.ShapeDtypeStruct(served.shape, bf1...  2.43 us

profile of v5, /device:TPU:25, one launch (start us, length us, event | category | flops | bytes accessed | tf_op | source)
XLA Modules:
  0.0 63.8 jit_solution(10380974165533826693)
XLA Ops:
  0.6 60.8 %exchange.1 = (bf16[1024,2048]{1,0:T(8,128)(2,1)S(1)}, bf16[256,8,256]{2,1,0:T(8,128)(2,1)S(1)}) custom-call(s32[2,128]{1,0:T(2,128)} %bitcast.3, bf16[256,2560]{1,0:T(8,128)(2,1)} %hidden_hbm.1, f32[1,256]{1,0:T(1,128)} %bitcast.4, bf16[2,4096,256]{2,1,0:T(8,128)(2,1)} %table_ref.1, bf16[2560,2048]{1,0:T(8,128)(2,1)} %w_ref.1), custom_call_target="tpu_custom_call" | custom-call | tf_op jit(solution)/shard_map/exchange/pallas_call | solution.py:433
  61.4 2.4 %put_out.1 = (bf16[1024,2048]{1,0:T(8,128)(2,1)}, bf16[256,8,256]{2,1,0:T(8,128)(2,1)}) custom-call(bf16[1024,2048]{1,0:T(8,128)(2,1)S(1)} %get-tuple-element.6.served_ref, bf16[256,8,256]{2,1,0:T(8,128)(2,1)S(1)} %get-tuple-element.7.mixed_ref), custom_call_target="tpu_custom_call" | custom-call | tf_op jit(solution)/shard_map/put_out/pallas_call | solution.py:471
